TPU v7x, 32 devices: a whole 2x2x4 slice. The times are simulated.
32 devices in a mesh: dom: 8 (over z, x), sub: 4 (over y, core).
Axes of the slice: x: 2, y: 2, z: 4, core: 2. Of those that a mesh axis runs over, the one named last changes fastest.
Arguments:
- level_set: float32 [64, 32, 128], P('dom', 'sub'), may hold values from 0 to 1
- velocity: float32 [3, 64, 32, 128], P(None, 'dom', 'sub'), may hold values from -6 to 6
- source: float32 [64, 32, 128], P('dom', 'sub'), may hold values from -12 to 12
Outputs:
- new_level: float32 [64, 32, 128], P('dom', 'sub')
- pressure: float32 [64, 32, 128], P('dom', 'sub')
- correction: float32 [64, 32, 128], P('dom', 'sub')
All inputs are finite; a program needn't handle non-finite values.
Results may differ from a plain program's by a relative error of at most 0.0003.
Values sent between devices are 32-bit elements; how exact they have to be, the bound alone decides.
A program may use at most 64 MiB of HBM per device.

v0:
```python
import math
import jax
import jax.numpy as jnp
import numpy as np
from jax import lax
from jax.sharding import PartitionSpec as P

SWEEPS = 2
PITERS = 2
gll_nodes = [
    -1.0,
    -0.8717401485096066,
    -0.5917001814331423,
    -0.2092992179024789,
    0.2092992179024789,
    0.5917001814331423,
    0.8717401485096066,
    1.0,
]
advect_step = 0.05
reinit_step = 0.02
interface_width = 0.1
density_ratio = 9.0


def padded(x, sides, width):
    for axis, dim in sides:
        devices, length = (lax.axis_size(axis), x.shape[dim])
        up = [(i, (i + 1) % devices) for i in range(devices)]
        down = [(j, i) for i, j in up]
        last = lax.slice_in_dim(x, length - width, length, axis=dim)
        leading = lax.slice_in_dim(x, 0, width, axis=dim)
        before = lax.ppermute(last, axis, up)
        after = lax.ppermute(leading, axis, down)
        x = jnp.concatenate([before, x, after], axis=dim)
    return x


def tables():
    node_points = np.array(gll_nodes)
    poly_order = 7
    values_prev = np.ones(8)
    values_now = node_points.copy()
    for degree in range(1, poly_order):
        values_next = ((2 * degree + 1) * node_points * values_now - degree * values_prev) / (
            degree + 1
        )
        values_prev, values_now = (values_now, values_next)
    matrix = np.zeros((8, 8))
    for line in range(8):
        for column in range(8):
            if line != column:
                matrix[line, column] = values_now[line] / (
                    values_now[column] * (node_points[line] - node_points[column])
                )
    matrix[0, 0] = -poly_order * (poly_order + 1) / 4.0
    matrix[7, 7] = poly_order * (poly_order + 1) / 4.0
    weights = 2.0 / (poly_order * (poly_order + 1) * values_now**2)
    return (matrix, weights)


def point_tables(full_shape, weights):
    corner_count = np.array([2.0, 1.0, 1.0, 1.0, 1.0, 1.0, 1.0, 2.0])
    weight_lines = []
    count_lines = []
    for dim_index in (1, 2, 3):
        repeats = full_shape[dim_index] // 8
        weight_lines.append(jnp.asarray(np.tile(weights, repeats), jnp.float32))
        count_lines.append(jnp.asarray(np.tile(1.0 / corner_count, repeats), jnp.float32))
    weight_cube = (
        weight_lines[0][:, None, None]
        * weight_lines[1][None, :, None]
        * weight_lines[2][None, None, :]
    )[None]
    inv_mult = (
        count_lines[0][:, None, None]
        * count_lines[1][None, :, None]
        * count_lines[2][None, None, :]
    )[None]
    return (weight_cube, inv_mult)


def derive(values, dim_index, matrix):
    full_shape = values.shape
    highest = lax.Precision.HIGHEST
    if dim_index == 1:
        blocks = values.reshape((full_shape[0], full_shape[1] // 8, 8) + full_shape[2:])
        result = jnp.einsum(
            "baipq,ji->bajpq", blocks, jnp.asarray(matrix, jnp.float32), precision=highest
        )
    elif dim_index == 2:
        blocks = values.reshape(full_shape[:2] + (full_shape[2] // 8, 8, full_shape[3]))
        result = jnp.einsum(
            "bpaiq,ji->bpajq", blocks, jnp.asarray(matrix, jnp.float32), precision=highest
        )
    else:
        block_width = math.gcd(full_shape[3], 128)
        block_matrix = jnp.asarray(np.kron(np.eye(block_width // 8), matrix), jnp.float32)
        blocks = values.reshape(full_shape[:3] + (full_shape[3] // block_width, block_width))
        result = jnp.einsum("bpqai,ji->bpqaj", blocks, block_matrix, precision=highest)
    return result.reshape(full_shape)


def gradient(values, matrix):
    return [derive(values, 1, matrix), derive(values, 2, matrix), derive(values, 3, matrix)]


def join_edges(values, upper, lower, dim_index):
    position = lax.broadcasted_iota(jnp.int32, values.shape, dim_index) % 8
    return values + jnp.where(position == 7, upper, 0.0) + jnp.where(position == 0, lower, 0.0)


def fold_faces(widened, dim_index, length):
    values = lax.slice_in_dim(widened, 1, length + 1, axis=dim_index)
    upper = lax.slice_in_dim(widened, 2, length + 2, axis=dim_index)
    lower = lax.slice_in_dim(widened, 0, length, axis=dim_index)
    return join_edges(values, upper, lower, dim_index)


def fold_local(values, dim_index):
    upper = jnp.roll(values, -1, axis=dim_index)
    lower = jnp.roll(values, 1, axis=dim_index)
    return join_edges(values, upper, lower, dim_index)


def assemble(values):
    widened = padded(values, (("dom", 1),), 1)
    values = fold_faces(widened, 1, values.shape[1])
    widened = padded(values, (("sub", 2),), 1)
    values = fold_faces(widened, 2, values.shape[2])
    return fold_local(values, 3)


def both_sums(residual, precond, applied, inv_mult):
    return lax.psum(
        (jnp.sum(residual * precond * inv_mult), jnp.sum(precond * applied * inv_mult)),
        ("dom", "sub"),
    )


def local(level_set, velocity, source):
    matrix, weights = tables()
    phase_field = level_set[None]
    weight_cube, inv_mult = point_tables(phase_field.shape, weights)
    gradients = gradient(phase_field, matrix)
    advected = phase_field - advect_step * (
        velocity[0:1] * gradients[0] + velocity[1:2] * gradients[1] + velocity[2:3] * gradients[2]
    )
    phase_field = assemble(advected) * inv_mult
    gradients = gradient(phase_field, matrix)
    magnitude = jnp.sqrt(
        gradients[0] * gradients[0] + gradients[1] * gradients[1] + gradients[2] * gradients[2]
    )
    scaled = 1.0 / jnp.maximum(magnitude, 1.0)
    normals = [gradients[0] * scaled, gradients[1] * scaled, gradients[2] * scaled]
    for sweep_index in range(SWEEPS):
        if sweep_index > 0:
            gradients = gradient(phase_field, matrix)
        compress = phase_field * (1.0 - phase_field)
        change = derive(interface_width * gradients[0] - compress * normals[0], 1, matrix)
        change = change + derive(interface_width * gradients[1] - compress * normals[1], 2, matrix)
        change = change + derive(interface_width * gradients[2] - compress * normals[2], 3, matrix)
        phase_field = phase_field + reinit_step * assemble(change) * inv_mult
    mobility = 1.0 / (1.0 + density_ratio * phase_field * phase_field)
    weighted = weight_cube * mobility
    square_t = (matrix * matrix).T
    diag_local = (
        weight_cube
        + derive(weighted, 1, square_t)
        + derive(weighted, 2, square_t)
        + derive(weighted, 3, square_t)
    )
    assembled = assemble(jnp.concatenate([weight_cube * source[None], diag_local], axis=0))
    right_side = assembled[0:1]
    diagonal = assembled[1:2]
    transposed = matrix.T

    def operate(direction):
        grads_dir = gradient(direction, matrix)
        local_sum = weight_cube * direction + derive(weighted * grads_dir[0], 1, transposed)
        local_sum = (
            local_sum
            + derive(weighted * grads_dir[1], 2, transposed)
            + derive(weighted * grads_dir[2], 3, transposed)
        )
        return assemble(local_sum)

    solution = jnp.zeros_like(right_side)
    residual = right_side
    precond = residual / diagonal
    applied = operate(precond)
    norm_now, product = both_sums(residual, precond, applied, inv_mult)
    step_size = norm_now / product
    direction = precond
    along_image = applied
    for step_index in range(PITERS):
        solution = solution + step_size * direction
        residual = residual - step_size * along_image
        if step_index + 1 < PITERS:
            precond = residual / diagonal
            applied = operate(precond)
            norm_next, product = both_sums(residual, precond, applied, inv_mult)
            ratio_new = norm_next / norm_now
            step_size = norm_next / (product - ratio_new * norm_next / step_size)
            direction = precond + ratio_new * direction
            along_image = applied + ratio_new * along_image
            norm_now = norm_next
    return (phase_field[0], solution[0], (residual / diagonal)[0])


def solution(mesh):
    return jax.shard_map(
        local,
        mesh=mesh,
        in_specs=(P("dom", "sub", None), P(None, "dom", "sub", None), P("dom", "sub", None)),
        out_specs=(P("dom", "sub", None), P("dom", "sub", None), P("dom", "sub", None)),
        check_vma=False,
    )
```

profile of v0, /device:TPU:14, one launch (start us, length us, event | category | flops | bytes accessed | tf_op | source)
XLA Modules:
  0.0 165.5 jit_solution(13758522378719981348)
XLA Ops:
  0.7 0.8 fusion.168
  3.3 2.4 %collective-permute-start.1 = (f32[1,1,8,128]{3,1,2,0:T(1,128)S(1)}, f32[1,1,8,128]{3,1,2,0:T(1,128)S(1)}, u32[]{:S(2)}, u32[]{:S(2)}) collective-permute-start(f32[1,1,8,128]{3,1,2,0:T(1,128)S(1)} %get-tuple-element.74), channel_id=1, source_target_pairs={{0,4},{4,8},{8,12},{12,16},{16,20},{20,24},{24,28},{28,0},{1,5},{5... | collective-permute-start | bytes 12296 | tf_op jit(solution)/shard_map/ppermute | solution.py:33
  6.5 0.8 collective-permute-done
  8.0 0.8 collective-permute-done.2
  8.8 1.8 %collective-permute-done.3 = f32[1,8,1,128]{3,1,2,0:T(8,128)S(1)} collective-permute-done((f32[1,8,1,128]{3,1,2,0:T(8,128)S(1)}, f32[1,8,1,128]{3,1,2,0:T(8,128)S(1)}, u32[]{:S(2)}, u32[]{:S(2)}) %collective-permute-start.3) | collective-permute-done | bytes 4128 | tf_op jit(solution)/shard_map/ppermute | solution.py:33
  12.8 2.0 %collective-permute-start.4 = (f32[1,1,8,128]{3,1,2,0:T(1,128)S(1)}, f32[1,1,8,128]{3,1,2,0:T(1,128)S(1)}, u32[]{:S(2)}, u32[]{:S(2)}) collective-permute-start(f32[1,1,8,128]{3,1,2,0:T(1,128)S(1)} %get-tuple-element.61), channel_id=1, source_target_pairs={{4,0},{8,4},{12,8},{16,12},{20,16},{24,20},{28,24},{0,28},{5,1},{9... | collective-permute-start | bytes 12296 | tf_op jit(solution)/shard_map/ppermute | solution.py:34
  14.8 1.1 collective-permute-start.5
  15.9 1.5 collective-permute-done.4
  17.4 1.1 collective-permute-done.5
  19.2 0.8 collective-permute-done.6
  20.0 1.8 %collective-permute-done.7 = f32[1,8,1,128]{3,1,2,0:T(8,128)S(1)} collective-permute-done((f32[1,8,1,128]{3,1,2,0:T(8,128)S(1)}, f32[1,8,1,128]{3,1,2,0:T(8,128)S(1)}, u32[]{:S(2)}, u32[]{:S(2)}) %collective-permute-start.7) | collective-permute-done | bytes 4128 | tf_op jit(solution)/shard_map/ppermute | solution.py:33
  23.4 4.8 %collective-permute-start.8 = (f32[1,1,8,128]{3,1,2,0:T(1,128)S(1)}, f32[1,1,8,128]{3,1,2,0:T(1,128)S(1)}, u32[]{:S(2)}, u32[]{:S(2)}) collective-permute-start(f32[1,1,8,128]{3,1,2,0:T(1,128)S(1)} %get-tuple-element.53), channel_id=1, source_target_pairs={{4,0},{8,4},{12,8},{16,12},{20,16},{24,20},{28,24},{0,28},{5,1},{9... | collective-permute-start | bytes 12296 | tf_op jit(solution)/shard_map/ppermute | solution.py:34
  28.2 1.2 collective-permute-done.8
  29.5 2.3 %collective-permute-done.9 = f32[1,1,8,128]{3,1,2,0:T(1,128)S(1)} collective-permute-done((f32[1,1,8,128]{3,1,2,0:T(1,128)S(1)}, f32[1,1,8,128]{3,1,2,0:T(1,128)S(1)}, u32[]{:S(2)}, u32[]{:S(2)}) %collective-permute-start.9) | collective-permute-done | bytes 4128 | tf_op jit(solution)/shard_map/ppermute | solution.py:33
  33.3 1.8 %collective-permute-done.11 = f32[1,8,1,128]{3,1,2,0:T(8,128)S(1)} collective-permute-done((f32[1,8,1,128]{3,1,2,0:T(8,128)S(1)}, f32[1,8,1,128]{3,1,2,0:T(8,128)S(1)}, u32[]{:S(2)}, u32[]{:S(2)}) %collective-permute-start.11) | collective-permute-done | bytes 4128 | tf_op jit(solution)/shard_map/ppermute | solution.py:33
  37.3 3.0 %collective-permute-start.12 = (f32[2,1,8,128]{3,1,2,0:T(1,128)S(1)}, f32[2,1,8,128]{3,1,2,0:T(1,128)S(1)}, u32[]{:S(2)}, u32[]{:S(2)}) collective-permute-start(f32[2,1,8,128]{3,1,2,0:T(1,128)S(1)} %get-tuple-element.29), channel_id=1, source_target_pairs={{4,0},{8,4},{12,8},{16,12},{20,16},{24,20},{28,24},{0,28},{5,1},{9... | collective-permute-start | bytes 24584 | tf_op jit(solution)/shard_map/ppermute | solution.py:34
  40.3 1.6 collective-permute-done.12
  41.9 2.0 %collective-permute-done.13 = f32[2,1,8,128]{3,1,2,0:T(1,128)S(1)} collective-permute-done((f32[2,1,8,128]{3,1,2,0:T(1,128)S(1)}, f32[2,1,8,128]{3,1,2,0:T(1,128)S(1)}, u32[]{:S(2)}, u32[]{:S(2)}) %collective-permute-start.13) | collective-permute-done | bytes 8224 | tf_op jit(solution)/shard_map/ppermute | solution.py:33
  44.6 0.9 collective-permute-done.14
  45.4 1.8 %collective-permute-done.15 = f32[2,8,1,128]{3,1,2,0:T(8,128)S(1)} collective-permute-done((f32[2,8,1,128]{3,1,2,0:T(8,128)S(1)}, f32[2,8,1,128]{3,1,2,0:T(8,128)S(1)}, u32[]{:S(2)}, u32[]{:S(2)}) %collective-permute-start.15) | collective-permute-done | bytes 8224 | tf_op jit(solution)/shard_map/ppermute | solution.py:33
  50.2 2.8 %collective-permute-start.16 = (f32[1,1,8,128]{3,1,2,0:T(1,128)S(1)}, f32[1,1,8,128]{3,1,2,0:T(1,128)S(1)}, u32[]{:S(2)}, u32[]{:S(2)}) collective-permute-start(f32[1,1,8,128]{3,1,2,0:T(1,128)S(1)} %get-tuple-element.45), channel_id=1, source_target_pairs={{4,0},{8,4},{12,8},{16,12},{20,16},{24,20},{28,24},{0,28},{5,1},{9... | collective-permute-start | bytes 12296 | tf_op jit(solution)/shard_map/ppermute | solution.py:34
  53.2 1.6 collective-permute-done.16
  54.7 1.9 %collective-permute-done.17 = f32[1,1,8,128]{3,1,2,0:T(1,128)S(1)} collective-permute-done((f32[1,1,8,128]{3,1,2,0:T(1,128)S(1)}, f32[1,1,8,128]{3,1,2,0:T(1,128)S(1)}, u32[]{:S(2)}, u32[]{:S(2)}) %collective-permute-start.17) | collective-permute-done | bytes 4128 | tf_op jit(solution)/shard_map/ppermute | solution.py:33
  57.3 0.8 collective-permute-done.18
  58.1 1.8 %collective-permute-done.19 = f32[1,8,1,128]{3,1,2,0:T(8,128)S(1)} collective-permute-done((f32[1,8,1,128]{3,1,2,0:T(8,128)S(1)}, f32[1,8,1,128]{3,1,2,0:T(8,128)S(1)}, u32[]{:S(2)}, u32[]{:S(2)}) %collective-permute-start.19) | collective-permute-done | bytes 4128 | tf_op jit(solution)/shard_map/ppermute | solution.py:33
  60.1 0.7 fusion.105
  60.8 44.3 %all-reduce.1 = (f32[]{:T(128)}, f32[]{:T(128)}) all-reduce(f32[]{:T(128)} %get-tuple-element.9, f32[]{:T(128)} %get-tuple-element.8), channel_id=1, replica_groups=mesh['dom'=8,'sub'=4] {'dom','sub'}, use_global_device_ids=true, to_apply=%region_1.2 | all-reduce | flops 2 | bytes 16 | tf_op jit(solution)/shard_map/psum | solution.py:135
  108.4 2.3 %collective-permute-start.21 = (f32[1,1,8,128]{3,1,2,0:T(1,128)S(1)}, f32[1,1,8,128]{3,1,2,0:T(1,128)S(1)}, u32[]{:S(2)}, u32[]{:S(2)}) collective-permute-start(f32[1,1,8,128]{3,1,2,0:T(1,128)S(1)} %get-tuple-element.38), channel_id=1, source_target_pairs={{0,4},{4,8},{8,12},{12,16},{16,20},{20,24},{24,28},{28,0},{1,5},{5... | collective-permute-start | bytes 12296 | tf_op jit(solution)/shard_map/ppermute | solution.py:33
  110.7 1.6 collective-permute-done.20
  113.8 1.8 %collective-permute-done.23 = f32[1,8,1,128]{3,1,2,0:T(8,128)S(1)} collective-permute-done((f32[1,8,1,128]{3,1,2,0:T(8,128)S(1)}, f32[1,8,1,128]{3,1,2,0:T(8,128)S(1)}, u32[]{:S(2)}, u32[]{:S(2)}) %collective-permute-start.23) | collective-permute-done | bytes 4128 | tf_op jit(solution)/shard_map/ppermute | solution.py:33
  115.8 0.8 fusion.107
  116.6 43.1 %all-reduce = (f32[]{:T(128)}, f32[]{:T(128)}) all-reduce(f32[]{:T(128)} %get-tuple-element.7, f32[]{:T(128)} %get-tuple-element.6), channel_id=1, replica_groups=mesh['dom'=8,'sub'=4] {'dom','sub'}, use_global_device_ids=true, to_apply=%region_5.6 | all-reduce | flops 2 | bytes 16 | tf_op jit(solution)/shard_map/psum | solution.py:135
  (136 shorter events, 20.8 us)
Async XLA Ops:
  0.6 0.8 copy-start.1
  0.6 0.8 copy-start.2
  1.6 0.9 copy-start
  2.8 4.6 %collective-permute-start = (f32[1,1,8,128]{3,1,2,0:T(1,128)S(1)}, f32[1,1,8,128]{3,1,2,0:T(1,128)S(1)}, u32[]{:S(2)}, u32[]{:S(2)}) collective-permute-start(f32[1,1,8,128]{3,1,2,0:T(1,128)S(1)} %get-tuple-element.73), channel_id=1, source_target_pairs={{4,0},{8,4},{12,8},{16,12},{20,16},{24,20},{28,24},{0,28},{5,1},{9... | collective-permute-start | bytes 12296 | tf_op jit(solution)/shard_map/ppermute | solution.py:34
  3.3 4.0 %collective-permute-start.1 = (f32[1,1,8,128]{3,1,2,0:T(1,128)S(1)}, f32[1,1,8,128]{3,1,2,0:T(1,128)S(1)}, u32[]{:S(2)}, u32[]{:S(2)}) collective-permute-start(f32[1,1,8,128]{3,1,2,0:T(1,128)S(1)} %get-tuple-element.74), channel_id=1, source_target_pairs={{0,4},{4,8},{8,12},{12,16},{16,20},{20,24},{24,28},{28,0},{1,5},{5... | collective-permute-start | bytes 12296 | tf_op jit(solution)/shard_map/ppermute | solution.py:33
  7.4 1.4 collective-permute-start.2
  7.5 3.1 %collective-permute-start.3 = (f32[1,8,1,128]{3,1,2,0:T(8,128)S(1)}, f32[1,8,1,128]{3,1,2,0:T(8,128)S(1)}, u32[]{:S(2)}, u32[]{:S(2)}) collective-permute-start(f32[1,8,1,128]{3,1,2,0:T(8,128)S(1)} %get-tuple-element.72), channel_id=1, source_target_pairs={{0,1},{1,2},{2,3},{3,0},{4,5},{5,6},{6,7},{7,4},{8,9},{9,10},{10,1... | collective-permute-start | bytes 12296 | tf_op jit(solution)/shard_map/ppermute | solution.py:33
  12.8 4.6 %collective-permute-start.4 = (f32[1,1,8,128]{3,1,2,0:T(1,128)S(1)}, f32[1,1,8,128]{3,1,2,0:T(1,128)S(1)}, u32[]{:S(2)}, u32[]{:S(2)}) collective-permute-start(f32[1,1,8,128]{3,1,2,0:T(1,128)S(1)} %get-tuple-element.61), channel_id=1, source_target_pairs={{4,0},{8,4},{12,8},{16,12},{20,16},{24,20},{28,24},{0,28},{5,1},{9... | collective-permute-start | bytes 12296 | tf_op jit(solution)/shard_map/ppermute | solution.py:34
  14.8 3.7 %collective-permute-start.5 = (f32[1,1,8,128]{3,1,2,0:T(1,128)S(1)}, f32[1,1,8,128]{3,1,2,0:T(1,128)S(1)}, u32[]{:S(2)}, u32[]{:S(2)}) collective-permute-start(f32[1,1,8,128]{3,1,2,0:T(1,128)S(1)} %get-tuple-element.62), channel_id=1, source_target_pairs={{0,4},{4,8},{8,12},{12,16},{16,20},{20,24},{24,28},{28,0},{1,5},{5... | collective-permute-start | bytes 12296 | tf_op jit(solution)/shard_map/ppermute | solution.py:33
  18.6 1.4 collective-permute-start.6
  18.7 3.1 %collective-permute-start.7 = (f32[1,8,1,128]{3,1,2,0:T(8,128)S(1)}, f32[1,8,1,128]{3,1,2,0:T(8,128)S(1)}, u32[]{:S(2)}, u32[]{:S(2)}) collective-permute-start(f32[1,8,1,128]{3,1,2,0:T(8,128)S(1)} %get-tuple-element.60), channel_id=1, source_target_pairs={{0,1},{1,2},{2,3},{3,0},{4,5},{5,6},{6,7},{7,4},{8,9},{9,10},{10,1... | collective-permute-start | bytes 12296 | tf_op jit(solution)/shard_map/ppermute | solution.py:33
  23.4 4.8 %copy-start.9 = (f32[8]{0:T(128)S(1)}, f32[8]{0:T(128)}, u32[]{:S(2)}) copy-start(f32[8]{0:T(128)} %constant.109.clone) | copy-start | bytes 100
  23.4 6.1 %collective-permute-start.8 = (f32[1,1,8,128]{3,1,2,0:T(1,128)S(1)}, f32[1,1,8,128]{3,1,2,0:T(1,128)S(1)}, u32[]{:S(2)}, u32[]{:S(2)}) collective-permute-start(f32[1,1,8,128]{3,1,2,0:T(1,128)S(1)} %get-tuple-element.53), channel_id=1, source_target_pairs={{4,0},{8,4},{12,8},{16,12},{20,16},{24,20},{28,24},{0,28},{5,1},{9... | collective-permute-start | bytes 12296 | tf_op jit(solution)/shard_map/ppermute | solution.py:34
  28.2 3.6 %collective-permute-start.9 = (f32[1,1,8,128]{3,1,2,0:T(1,128)S(1)}, f32[1,1,8,128]{3,1,2,0:T(1,128)S(1)}, u32[]{:S(2)}, u32[]{:S(2)}) collective-permute-start(f32[1,1,8,128]{3,1,2,0:T(1,128)S(1)} %get-tuple-element.54), channel_id=1, source_target_pairs={{0,4},{4,8},{8,12},{12,16},{16,20},{20,24},{24,28},{28,0},{1,5},{5... | collective-permute-start | bytes 12296 | tf_op jit(solution)/shard_map/ppermute | solution.py:33
  28.2 4.2 %copy-start.5 = (f32[8,8,128]{2,1,0:T(8,128)S(1)}, f32[8,8,128]{2,1,0:T(8,128)}, u32[]{:S(2)}) copy-start(f32[8,8,128]{2,1,0:T(8,128)} %param.41) | copy-start | bytes 98308
  31.9 1.4 collective-permute-start.10
  31.9 3.1 %collective-permute-start.11 = (f32[1,8,1,128]{3,1,2,0:T(8,128)S(1)}, f32[1,8,1,128]{3,1,2,0:T(8,128)S(1)}, u32[]{:S(2)}, u32[]{:S(2)}) collective-permute-start(f32[1,8,1,128]{3,1,2,0:T(8,128)S(1)} %get-tuple-element.52), channel_id=1, source_target_pairs={{0,1},{1,2},{2,3},{3,0},{4,5},{5,6},{6,7},{7,4},{8,9},{9,10},{10,1... | collective-permute-start | bytes 12296 | tf_op jit(solution)/shard_map/ppermute | solution.py:33
  36.1 0.9 copy-start.11
  37.3 4.6 %collective-permute-start.12 = (f32[2,1,8,128]{3,1,2,0:T(1,128)S(1)}, f32[2,1,8,128]{3,1,2,0:T(1,128)S(1)}, u32[]{:S(2)}, u32[]{:S(2)}) collective-permute-start(f32[2,1,8,128]{3,1,2,0:T(1,128)S(1)} %get-tuple-element.29), channel_id=1, source_target_pairs={{4,0},{8,4},{12,8},{16,12},{20,16},{24,20},{28,24},{0,28},{5,1},{9... | collective-permute-start | bytes 24584 | tf_op jit(solution)/shard_map/ppermute | solution.py:34
  40.3 3.7 %collective-permute-start.13 = (f32[2,1,8,128]{3,1,2,0:T(1,128)S(1)}, f32[2,1,8,128]{3,1,2,0:T(1,128)S(1)}, u32[]{:S(2)}, u32[]{:S(2)}) collective-permute-start(f32[2,1,8,128]{3,1,2,0:T(1,128)S(1)} %get-tuple-element.30), channel_id=1, source_target_pairs={{0,4},{4,8},{8,12},{12,16},{16,20},{20,24},{24,28},{28,0},{1,5},{5... | collective-permute-start | bytes 24584 | tf_op jit(solution)/shard_map/ppermute | solution.py:33
  44.0 1.4 collective-permute-start.14
  44.1 3.1 %collective-permute-start.15 = (f32[2,8,1,128]{3,1,2,0:T(8,128)S(1)}, f32[2,8,1,128]{3,1,2,0:T(8,128)S(1)}, u32[]{:S(2)}, u32[]{:S(2)}) collective-permute-start(f32[2,8,1,128]{3,1,2,0:T(8,128)S(1)} %get-tuple-element.28), channel_id=1, source_target_pairs={{0,1},{1,2},{2,3},{3,0},{4,5},{5,6},{6,7},{7,4},{8,9},{9,10},{10,1... | collective-permute-start | bytes 24584 | tf_op jit(solution)/shard_map/ppermute | solution.py:33
  48.2 0.7 copy-start.4
  49.1 0.8 copy-start.3
  50.2 4.6 %collective-permute-start.16 = (f32[1,1,8,128]{3,1,2,0:T(1,128)S(1)}, f32[1,1,8,128]{3,1,2,0:T(1,128)S(1)}, u32[]{:S(2)}, u32[]{:S(2)}) collective-permute-start(f32[1,1,8,128]{3,1,2,0:T(1,128)S(1)} %get-tuple-element.45), channel_id=1, source_target_pairs={{4,0},{8,4},{12,8},{16,12},{20,16},{24,20},{28,24},{0,28},{5,1},{9... | collective-permute-start | bytes 12296 | tf_op jit(solution)/shard_map/ppermute | solution.py:34
  53.0 3.6 %collective-permute-start.17 = (f32[1,1,8,128]{3,1,2,0:T(1,128)S(1)}, f32[1,1,8,128]{3,1,2,0:T(1,128)S(1)}, u32[]{:S(2)}, u32[]{:S(2)}) collective-permute-start(f32[1,1,8,128]{3,1,2,0:T(1,128)S(1)} %get-tuple-element.46), channel_id=1, source_target_pairs={{0,4},{4,8},{8,12},{12,16},{16,20},{20,24},{24,28},{28,0},{1,5},{5... | collective-permute-start | bytes 12296 | tf_op jit(solution)/shard_map/ppermute | solution.py:33
  56.7 1.4 collective-permute-start.18
  56.8 3.1 %collective-permute-start.19 = (f32[1,8,1,128]{3,1,2,0:T(8,128)S(1)}, f32[1,8,1,128]{3,1,2,0:T(8,128)S(1)}, u32[]{:S(2)}, u32[]{:S(2)}) collective-permute-start(f32[1,8,1,128]{3,1,2,0:T(8,128)S(1)} %get-tuple-element.44), channel_id=1, source_target_pairs={{0,1},{1,2},{2,3},{3,0},{4,5},{5,6},{6,7},{7,4},{8,9},{9,10},{10,1... | collective-permute-start | bytes 12296 | tf_op jit(solution)/shard_map/ppermute | solution.py:33
  107.7 4.6 %collective-permute-start.20 = (f32[1,1,8,128]{3,1,2,0:T(1,128)S(1)}, f32[1,1,8,128]{3,1,2,0:T(1,128)S(1)}, u32[]{:S(2)}, u32[]{:S(2)}) collective-permute-start(f32[1,1,8,128]{3,1,2,0:T(1,128)S(1)} %get-tuple-element.37), channel_id=1, source_target_pairs={{4,0},{8,4},{12,8},{16,12},{20,16},{24,20},{28,24},{0,28},{5,1},{9... | collective-permute-start | bytes 12296 | tf_op jit(solution)/shard_map/ppermute | solution.py:34
  108.4 3.9 %collective-permute-start.21 = (f32[1,1,8,128]{3,1,2,0:T(1,128)S(1)}, f32[1,1,8,128]{3,1,2,0:T(1,128)S(1)}, u32[]{:S(2)}, u32[]{:S(2)}) collective-permute-start(f32[1,1,8,128]{3,1,2,0:T(1,128)S(1)} %get-tuple-element.38), channel_id=1, source_target_pairs={{0,4},{4,8},{8,12},{12,16},{16,20},{20,24},{24,28},{28,0},{1,5},{5... | collective-permute-start | bytes 12296 | tf_op jit(solution)/shard_map/ppermute | solution.py:33
  112.4 1.4 collective-permute-start.22
  112.5 3.1 %collective-permute-start.23 = (f32[1,8,1,128]{3,1,2,0:T(8,128)S(1)}, f32[1,8,1,128]{3,1,2,0:T(8,128)S(1)}, u32[]{:S(2)}, u32[]{:S(2)}) collective-permute-start(f32[1,8,1,128]{3,1,2,0:T(8,128)S(1)} %get-tuple-element.36), channel_id=1, source_target_pairs={{0,1},{1,2},{2,3},{3,0},{4,5},{5,6},{6,7},{7,4},{8,9},{9,10},{10,1... | collective-permute-start | bytes 12296 | tf_op jit(solution)/shard_map/ppermute | solution.py:33
  (4 other events, 2.7 us)
where the time goes:
time: 166 us
  blocking collectives  87.4 us (53%)
  waiting for transfers between devices  30.5 us (18%)
  starting transfers between devices  23.1 us (14%)
  local copies, waits for them, and re-layouts  8.16 us (5%)
  between operations  7.03 us (4%)
  matrix products  5.75 us (3%)
  other arithmetic  3.65 us (2%)
    psum x2, blocking collectives, both_sums(): lax.psum((jnp.sum(residual * precond * inv_mult), jnp.sum(precond * appli...  87.4 us
    ppermute x12, waiting for transfers between devices, padded(): before = lax.ppermute(last, axis, up)  17.9 us
    ppermute x12, starting transfers between devices, padded(): after = lax.ppermute(leading, axis, down)  14.1 us
    ppermute x12, waiting for transfers between devices, padded(): after = lax.ppermute(leading, axis, down)  12.6 us
    ppermute x12, starting transfers between devices, padded(): before = lax.ppermute(last, axis, up)  8.96 us
    unnamed x27, local copies, waits for them, and re-layouts  6.39 us
  transfers between devices with their start and end apart: 24, of which 22 were waited for; matrix products, arithmetic and copies ran while one was open for 1% of the time, Pallas kernels for 0%

commit v1 on v0

--- a/solution.py
+++ b/solution.py
@@ -133,8 +133,10 @@
 
 def both_sums(residual, precond, applied, inv_mult):
     return lax.psum(
-        (jnp.sum(residual * precond * inv_mult), jnp.sum(precond * applied * inv_mult)),
-        ("dom", "sub"),
+        lax.psum(
+            (jnp.sum(residual * precond * inv_mult), jnp.sum(precond * applied * inv_mult)), "sub"
+        ),
+        "dom",
     )
 
 

time: 166 us -> 137 us (0.83)
  the two profiles are of different devices: /device:TPU:14 before, /device:TPU:0 now
where the time goes in v1:
time: 137 us
  blocking collectives  48.3 us (35%)
  waiting for transfers between devices  44.1 us (32%)
  starting transfers between devices  19.8 us (14%)
  local copies, waits for them, and re-layouts  8.15 us (6%)
  between operations  7.11 us (5%)
  matrix products  5.75 us (4%)
  other arithmetic  3.64 us (3%)
    psum x2, blocking collectives, both_sums(): lax.psum(lax.psum((jnp.sum(residual * precond * inv_mult), jnp.sum(precon...  35.6 us
    ppermute x12, waiting for transfers between devices, padded(): before = lax.ppermute(last, axis, up)  31.5 us
    psum x2, blocking collectives, both_sums(): lax.psum((jnp.sum(residual * precond * inv_mult), jnp.sum(precond * appli...  12.7 us
    ppermute x12, waiting for transfers between devices, padded(): after = lax.ppermute(leading, axis, down)  12.6 us
    ppermute x12, starting transfers between devices, padded(): before = lax.ppermute(last, axis, up)  11.1 us
    ppermute x12, starting transfers between devices, padded(): after = lax.ppermute(leading, axis, down)  8.7 us
    unnamed x27, local copies, waits for them, and re-layouts  6.38 us
  transfers between devices with their start and end apart: 24, of which 24 were waited for; matrix products, arithmetic and copies ran while one was open for 1% of the time, Pallas kernels for 0%

profile of v1, /device:TPU:0, one launch (start us, length us, event | category | flops | bytes accessed | tf_op | source)
XLA Modules:
  0.0 136.8 jit_solution(3530592171231972930)
XLA Ops:
  0.7 0.8 fusion.168
  2.7 6.1 %collective-permute-start = (f32[1,1,8,128]{3,1,2,0:T(1,128)S(1)}, f32[1,1,8,128]{3,1,2,0:T(1,128)S(1)}, u32[]{:S(2)}, u32[]{:S(2)}) collective-permute-start(f32[1,1,8,128]{3,1,2,0:T(1,128)S(1)} %get-tuple-element.77), channel_id=1, source_target_pairs={{4,0},{8,4},{12,8},{16,12},{20,16},{24,20},{28,24},{0,28},{5,1},{9... | collective-permute-start | bytes 12296 | tf_op jit(solution)/shard_map/ppermute | solution.py:34
  10.1 5.0 %collective-permute-done.1 = f32[1,1,8,128]{3,1,2,0:T(1,128)S(1)} collective-permute-done((f32[1,1,8,128]{3,1,2,0:T(1,128)S(1)}, f32[1,1,8,128]{3,1,2,0:T(1,128)S(1)}, u32[]{:S(2)}, u32[]{:S(2)}) %collective-permute-start.1) | collective-permute-done | bytes 4128 | tf_op jit(solution)/shard_map/ppermute | solution.py:33
  15.8 0.8 collective-permute-done.2
  16.6 1.8 %collective-permute-done.3 = f32[1,8,1,128]{3,1,2,0:T(8,128)S(1)} collective-permute-done((f32[1,8,1,128]{3,1,2,0:T(8,128)S(1)}, f32[1,8,1,128]{3,1,2,0:T(8,128)S(1)}, u32[]{:S(2)}, u32[]{:S(2)}) %collective-permute-start.3) | collective-permute-done | bytes 4128 | tf_op jit(solution)/shard_map/ppermute | solution.py:33
  20.7 2.0 %collective-permute-start.5 = (f32[1,1,8,128]{3,1,2,0:T(1,128)S(1)}, f32[1,1,8,128]{3,1,2,0:T(1,128)S(1)}, u32[]{:S(2)}, u32[]{:S(2)}) collective-permute-start(f32[1,1,8,128]{3,1,2,0:T(1,128)S(1)} %get-tuple-element.66), channel_id=1, source_target_pairs={{0,4},{4,8},{8,12},{12,16},{16,20},{20,24},{24,28},{28,0},{1,5},{5... | collective-permute-start | bytes 12296 | tf_op jit(solution)/shard_map/ppermute | solution.py:33
  22.8 1.6 %collective-permute-done.4 = f32[1,1,8,128]{3,1,2,0:T(1,128)S(1)} collective-permute-done((f32[1,1,8,128]{3,1,2,0:T(1,128)S(1)}, f32[1,1,8,128]{3,1,2,0:T(1,128)S(1)}, u32[]{:S(2)}, u32[]{:S(2)}) %collective-permute-start.4) | collective-permute-done | bytes 4128 | tf_op jit(solution)/shard_map/ppermute | solution.py:34
  24.3 2.8 %collective-permute-done.5 = f32[1,1,8,128]{3,1,2,0:T(1,128)S(1)} collective-permute-done((f32[1,1,8,128]{3,1,2,0:T(1,128)S(1)}, f32[1,1,8,128]{3,1,2,0:T(1,128)S(1)}, u32[]{:S(2)}, u32[]{:S(2)}) %collective-permute-start.5) | collective-permute-done | bytes 4128 | tf_op jit(solution)/shard_map/ppermute | solution.py:33
  27.7 0.8 collective-permute-done.6
  28.6 1.8 %collective-permute-done.7 = f32[1,8,1,128]{3,1,2,0:T(8,128)S(1)} collective-permute-done((f32[1,8,1,128]{3,1,2,0:T(8,128)S(1)}, f32[1,8,1,128]{3,1,2,0:T(8,128)S(1)}, u32[]{:S(2)}, u32[]{:S(2)}) %collective-permute-start.7) | collective-permute-done | bytes 4128 | tf_op jit(solution)/shard_map/ppermute | solution.py:33
  32.1 2.0 %collective-permute-start.9 = (f32[1,1,8,128]{3,1,2,0:T(1,128)S(1)}, f32[1,1,8,128]{3,1,2,0:T(1,128)S(1)}, u32[]{:S(2)}, u32[]{:S(2)}) collective-permute-start(f32[1,1,8,128]{3,1,2,0:T(1,128)S(1)} %get-tuple-element.58), channel_id=1, source_target_pairs={{0,4},{4,8},{8,12},{12,16},{16,20},{20,24},{24,28},{28,0},{1,5},{5... | collective-permute-start | bytes 12296 | tf_op jit(solution)/shard_map/ppermute | solution.py:33
  34.1 1.5 %collective-permute-done.8 = f32[1,1,8,128]{3,1,2,0:T(1,128)S(1)} collective-permute-done((f32[1,1,8,128]{3,1,2,0:T(1,128)S(1)}, f32[1,1,8,128]{3,1,2,0:T(1,128)S(1)}, u32[]{:S(2)}, u32[]{:S(2)}) %collective-permute-start.8) | collective-permute-done | bytes 4128 | tf_op jit(solution)/shard_map/ppermute | solution.py:34
  35.6 2.8 %collective-permute-done.9 = f32[1,1,8,128]{3,1,2,0:T(1,128)S(1)} collective-permute-done((f32[1,1,8,128]{3,1,2,0:T(1,128)S(1)}, f32[1,1,8,128]{3,1,2,0:T(1,128)S(1)}, u32[]{:S(2)}, u32[]{:S(2)}) %collective-permute-start.9) | collective-permute-done | bytes 4128 | tf_op jit(solution)/shard_map/ppermute | solution.py:33
  39.9 1.8 %collective-permute-done.11 = f32[1,8,1,128]{3,1,2,0:T(8,128)S(1)} collective-permute-done((f32[1,8,1,128]{3,1,2,0:T(8,128)S(1)}, f32[1,8,1,128]{3,1,2,0:T(8,128)S(1)}, u32[]{:S(2)}, u32[]{:S(2)}) %collective-permute-start.11) | collective-permute-done | bytes 4128 | tf_op jit(solution)/shard_map/ppermute | solution.py:33
  44.0 2.0 %collective-permute-start.13 = (f32[2,1,8,128]{3,1,2,0:T(1,128)S(1)}, f32[2,1,8,128]{3,1,2,0:T(1,128)S(1)}, u32[]{:S(2)}, u32[]{:S(2)}) collective-permute-start(f32[2,1,8,128]{3,1,2,0:T(1,128)S(1)} %get-tuple-element.34), channel_id=1, source_target_pairs={{0,4},{4,8},{8,12},{12,16},{16,20},{20,24},{24,28},{28,0},{1,5},{5... | collective-permute-start | bytes 24584 | tf_op jit(solution)/shard_map/ppermute | solution.py:33
  46.0 1.6 %collective-permute-done.12 = f32[2,1,8,128]{3,1,2,0:T(1,128)S(1)} collective-permute-done((f32[2,1,8,128]{3,1,2,0:T(1,128)S(1)}, f32[2,1,8,128]{3,1,2,0:T(1,128)S(1)}, u32[]{:S(2)}, u32[]{:S(2)}) %collective-permute-start.12) | collective-permute-done | bytes 8224 | tf_op jit(solution)/shard_map/ppermute | solution.py:34
  47.6 2.8 %collective-permute-done.13 = f32[2,1,8,128]{3,1,2,0:T(1,128)S(1)} collective-permute-done((f32[2,1,8,128]{3,1,2,0:T(1,128)S(1)}, f32[2,1,8,128]{3,1,2,0:T(1,128)S(1)}, u32[]{:S(2)}, u32[]{:S(2)}) %collective-permute-start.13) | collective-permute-done | bytes 8224 | tf_op jit(solution)/shard_map/ppermute | solution.py:33
  51.0 0.9 collective-permute-done.14
  51.9 1.8 %collective-permute-done.15 = f32[2,8,1,128]{3,1,2,0:T(8,128)S(1)} collective-permute-done((f32[2,8,1,128]{3,1,2,0:T(8,128)S(1)}, f32[2,8,1,128]{3,1,2,0:T(8,128)S(1)}, u32[]{:S(2)}, u32[]{:S(2)}) %collective-permute-start.15) | collective-permute-done | bytes 8224 | tf_op jit(solution)/shard_map/ppermute | solution.py:33
  56.8 2.0 %collective-permute-start.17 = (f32[1,1,8,128]{3,1,2,0:T(1,128)S(1)}, f32[1,1,8,128]{3,1,2,0:T(1,128)S(1)}, u32[]{:S(2)}, u32[]{:S(2)}) collective-permute-start(f32[1,1,8,128]{3,1,2,0:T(1,128)S(1)} %get-tuple-element.50), channel_id=1, source_target_pairs={{0,4},{4,8},{8,12},{12,16},{16,20},{20,24},{24,28},{28,0},{1,5},{5... | collective-permute-start | bytes 12296 | tf_op jit(solution)/shard_map/ppermute | solution.py:33
  58.8 1.6 %collective-permute-done.16 = f32[1,1,8,128]{3,1,2,0:T(1,128)S(1)} collective-permute-done((f32[1,1,8,128]{3,1,2,0:T(1,128)S(1)}, f32[1,1,8,128]{3,1,2,0:T(1,128)S(1)}, u32[]{:S(2)}, u32[]{:S(2)}) %collective-permute-start.16) | collective-permute-done | bytes 4128 | tf_op jit(solution)/shard_map/ppermute | solution.py:34
  60.4 2.8 %collective-permute-done.17 = f32[1,1,8,128]{3,1,2,0:T(1,128)S(1)} collective-permute-done((f32[1,1,8,128]{3,1,2,0:T(1,128)S(1)}, f32[1,1,8,128]{3,1,2,0:T(1,128)S(1)}, u32[]{:S(2)}, u32[]{:S(2)}) %collective-permute-start.17) | collective-permute-done | bytes 4128 | tf_op jit(solution)/shard_map/ppermute | solution.py:33
  63.8 0.8 collective-permute-done.18
  64.6 1.8 %collective-permute-done.19 = f32[1,8,1,128]{3,1,2,0:T(8,128)S(1)} collective-permute-done((f32[1,8,1,128]{3,1,2,0:T(8,128)S(1)}, f32[1,8,1,128]{3,1,2,0:T(8,128)S(1)}, u32[]{:S(2)}, u32[]{:S(2)}) %collective-permute-start.19) | collective-permute-done | bytes 4128 | tf_op jit(solution)/shard_map/ppermute | solution.py:33
  67.3 6.3 %all-reduce.3 = (f32[]{:T(128)}, f32[]{:T(128)}) all-reduce(f32[]{:T(128)} %get-tuple-element.9, f32[]{:T(128)} %get-tuple-element.8), channel_id=1, replica_groups=mesh['dom'=8,'sub'=4] {'sub'}, use_global_device_ids=true, to_apply=%region_1.2 | all-reduce | flops 2 | bytes 16 | tf_op jit(solution)/shard_map/psum | solution.py:136
  73.6 17.8 %all-reduce.1 = (f32[]{:T(128)}, f32[]{:T(128)}) all-reduce(f32[]{:T(128)} %get-tuple-element.16, f32[]{:T(128)} %get-tuple-element.17), channel_id=1, replica_groups=mesh['dom'=8,'sub'=4] {'dom'}, use_global_device_ids=true, to_apply=%region_2.3 | all-reduce | flops 2 | bytes 16 | tf_op jit(solution)/shard_map/psum | solution.py:135
  94.0 2.1 %collective-permute-start.20 = (f32[1,1,8,128]{3,1,2,0:T(1,128)S(1)}, f32[1,1,8,128]{3,1,2,0:T(1,128)S(1)}, u32[]{:S(2)}, u32[]{:S(2)}) collective-permute-start(f32[1,1,8,128]{3,1,2,0:T(1,128)S(1)} %get-tuple-element.41), channel_id=1, source_target_pairs={{4,0},{8,4},{12,8},{16,12},{20,16},{24,20},{28,24},{0,28},{5,1},{9... | collective-permute-start | bytes 12296 | tf_op jit(solution)/shard_map/ppermute | solution.py:34
  96.1 1.5 %collective-permute-done.20 = f32[1,1,8,128]{3,1,2,0:T(1,128)S(1)} collective-permute-done((f32[1,1,8,128]{3,1,2,0:T(1,128)S(1)}, f32[1,1,8,128]{3,1,2,0:T(1,128)S(1)}, u32[]{:S(2)}, u32[]{:S(2)}) %collective-permute-start.20) | collective-permute-done | bytes 4128 | tf_op jit(solution)/shard_map/ppermute | solution.py:34
  97.7 4.7 %collective-permute-done.21 = f32[1,1,8,128]{3,1,2,0:T(1,128)S(1)} collective-permute-done((f32[1,1,8,128]{3,1,2,0:T(1,128)S(1)}, f32[1,1,8,128]{3,1,2,0:T(1,128)S(1)}, u32[]{:S(2)}, u32[]{:S(2)}) %collective-permute-start.21) | collective-permute-done | bytes 4128 | tf_op jit(solution)/shard_map/ppermute | solution.py:33
  103.8 1.8 %collective-permute-done.23 = f32[1,8,1,128]{3,1,2,0:T(8,128)S(1)} collective-permute-done((f32[1,8,1,128]{3,1,2,0:T(8,128)S(1)}, f32[1,8,1,128]{3,1,2,0:T(8,128)S(1)}, u32[]{:S(2)}, u32[]{:S(2)}) %collective-permute-start.23) | collective-permute-done | bytes 4128 | tf_op jit(solution)/shard_map/ppermute | solution.py:33
  106.7 6.4 %all-reduce.2 = (f32[]{:T(128)}, f32[]{:T(128)}) all-reduce(f32[]{:T(128)} %get-tuple-element.7, f32[]{:T(128)} %get-tuple-element.6), channel_id=1, replica_groups=mesh['dom'=8,'sub'=4] {'sub'}, use_global_device_ids=true, to_apply=%region_7.8 | all-reduce | flops 2 | bytes 16 | tf_op jit(solution)/shard_map/psum | solution.py:136
  113.1 17.8 %all-reduce = (f32[]{:T(128)}, f32[]{:T(128)}) all-reduce(f32[]{:T(128)} %get-tuple-element.14, f32[]{:T(128)} %get-tuple-element.15), channel_id=1, replica_groups=mesh['dom'=8,'sub'=4] {'dom'}, use_global_device_ids=true, to_apply=%region_8.9 | all-reduce | flops 2 | bytes 16 | tf_op jit(solution)/shard_map/psum | solution.py:135
  (138 shorter events, 21.8 us)
Async XLA Ops:
  0.6 0.8 copy-start.1
  0.6 0.8 copy-start.2
  1.6 0.8 copy-start
  2.7 7.4 %collective-permute-start = (f32[1,1,8,128]{3,1,2,0:T(1,128)S(1)}, f32[1,1,8,128]{3,1,2,0:T(1,128)S(1)}, u32[]{:S(2)}, u32[]{:S(2)}) collective-permute-start(f32[1,1,8,128]{3,1,2,0:T(1,128)S(1)} %get-tuple-element.77), channel_id=1, source_target_pairs={{4,0},{8,4},{12,8},{16,12},{20,16},{24,20},{28,24},{0,28},{5,1},{9... | collective-permute-start | bytes 12296 | tf_op jit(solution)/shard_map/ppermute | solution.py:34
  8.8 6.3 %collective-permute-start.1 = (f32[1,1,8,128]{3,1,2,0:T(1,128)S(1)}, f32[1,1,8,128]{3,1,2,0:T(1,128)S(1)}, u32[]{:S(2)}, u32[]{:S(2)}) collective-permute-start(f32[1,1,8,128]{3,1,2,0:T(1,128)S(1)} %get-tuple-element.78), channel_id=1, source_target_pairs={{0,4},{4,8},{8,12},{12,16},{16,20},{20,24},{24,28},{28,0},{1,5},{5... | collective-permute-start | bytes 12296 | tf_op jit(solution)/shard_map/ppermute | solution.py:33
  15.2 1.4 %collective-permute-start.2 = (f32[1,8,1,128]{3,1,2,0:T(8,128)S(1)}, f32[1,8,1,128]{3,1,2,0:T(8,128)S(1)}, u32[]{:S(2)}, u32[]{:S(2)}) collective-permute-start(f32[1,8,1,128]{3,1,2,0:T(8,128)S(1)} %get-tuple-element.75), channel_id=1, source_target_pairs={{1,0},{2,1},{3,2},{0,3},{5,4},{6,5},{7,6},{4,7},{9,8},{10,9},{11,1... | collective-permute-start | bytes 12296 | tf_op jit(solution)/shard_map/ppermute | solution.py:34
  15.3 3.1 %collective-permute-start.3 = (f32[1,8,1,128]{3,1,2,0:T(8,128)S(1)}, f32[1,8,1,128]{3,1,2,0:T(8,128)S(1)}, u32[]{:S(2)}, u32[]{:S(2)}) collective-permute-start(f32[1,8,1,128]{3,1,2,0:T(8,128)S(1)} %get-tuple-element.76), channel_id=1, source_target_pairs={{0,1},{1,2},{2,3},{3,0},{4,5},{5,6},{6,7},{7,4},{8,9},{9,10},{10,1... | collective-permute-start | bytes 12296 | tf_op jit(solution)/shard_map/ppermute | solution.py:33
  20.7 3.7 %collective-permute-start.4 = (f32[1,1,8,128]{3,1,2,0:T(1,128)S(1)}, f32[1,1,8,128]{3,1,2,0:T(1,128)S(1)}, u32[]{:S(2)}, u32[]{:S(2)}) collective-permute-start(f32[1,1,8,128]{3,1,2,0:T(1,128)S(1)} %get-tuple-element.65), channel_id=1, source_target_pairs={{4,0},{8,4},{12,8},{16,12},{20,16},{24,20},{28,24},{0,28},{5,1},{9... | collective-permute-start | bytes 12296 | tf_op jit(solution)/shard_map/ppermute | solution.py:34
  20.7 6.4 %collective-permute-start.5 = (f32[1,1,8,128]{3,1,2,0:T(1,128)S(1)}, f32[1,1,8,128]{3,1,2,0:T(1,128)S(1)}, u32[]{:S(2)}, u32[]{:S(2)}) collective-permute-start(f32[1,1,8,128]{3,1,2,0:T(1,128)S(1)} %get-tuple-element.66), channel_id=1, source_target_pairs={{0,4},{4,8},{8,12},{12,16},{16,20},{20,24},{24,28},{28,0},{1,5},{5... | collective-permute-start | bytes 12296 | tf_op jit(solution)/shard_map/ppermute | solution.py:33
  27.2 1.4 %collective-permute-start.6 = (f32[1,8,1,128]{3,1,2,0:T(8,128)S(1)}, f32[1,8,1,128]{3,1,2,0:T(8,128)S(1)}, u32[]{:S(2)}, u32[]{:S(2)}) collective-permute-start(f32[1,8,1,128]{3,1,2,0:T(8,128)S(1)} %get-tuple-element.63), channel_id=1, source_target_pairs={{1,0},{2,1},{3,2},{0,3},{5,4},{6,5},{7,6},{4,7},{9,8},{10,9},{11,1... | collective-permute-start | bytes 12296 | tf_op jit(solution)/shard_map/ppermute | solution.py:34
  27.3 3.1 %collective-permute-start.7 = (f32[1,8,1,128]{3,1,2,0:T(8,128)S(1)}, f32[1,8,1,128]{3,1,2,0:T(8,128)S(1)}, u32[]{:S(2)}, u32[]{:S(2)}) collective-permute-start(f32[1,8,1,128]{3,1,2,0:T(8,128)S(1)} %get-tuple-element.64), channel_id=1, source_target_pairs={{0,1},{1,2},{2,3},{3,0},{4,5},{5,6},{6,7},{7,4},{8,9},{9,10},{10,1... | collective-permute-start | bytes 12296 | tf_op jit(solution)/shard_map/ppermute | solution.py:33
  32.0 2.1 %copy-start.9 = (f32[8]{0:T(128)S(1)}, f32[8]{0:T(128)}, u32[]{:S(2)}) copy-start(f32[8]{0:T(128)} %constant.109.clone) | copy-start | bytes 100
  32.0 3.7 %collective-permute-start.8 = (f32[1,1,8,128]{3,1,2,0:T(1,128)S(1)}, f32[1,1,8,128]{3,1,2,0:T(1,128)S(1)}, u32[]{:S(2)}, u32[]{:S(2)}) collective-permute-start(f32[1,1,8,128]{3,1,2,0:T(1,128)S(1)} %get-tuple-element.57), channel_id=1, source_target_pairs={{4,0},{8,4},{12,8},{16,12},{20,16},{24,20},{28,24},{0,28},{5,1},{9... | collective-permute-start | bytes 12296 | tf_op jit(solution)/shard_map/ppermute | solution.py:34
  32.1 6.4 %collective-permute-start.9 = (f32[1,1,8,128]{3,1,2,0:T(1,128)S(1)}, f32[1,1,8,128]{3,1,2,0:T(1,128)S(1)}, u32[]{:S(2)}, u32[]{:S(2)}) collective-permute-start(f32[1,1,8,128]{3,1,2,0:T(1,128)S(1)} %get-tuple-element.58), channel_id=1, source_target_pairs={{0,4},{4,8},{8,12},{12,16},{16,20},{20,24},{24,28},{28,0},{1,5},{5... | collective-permute-start | bytes 12296 | tf_op jit(solution)/shard_map/ppermute | solution.py:33
  34.1 4.9 %copy-start.5 = (f32[8,8,128]{2,1,0:T(8,128)S(1)}, f32[8,8,128]{2,1,0:T(8,128)}, u32[]{:S(2)}) copy-start(f32[8,8,128]{2,1,0:T(8,128)} %param.41) | copy-start | bytes 98308
  38.5 1.4 %collective-permute-start.10 = (f32[1,8,1,128]{3,1,2,0:T(8,128)S(1)}, f32[1,8,1,128]{3,1,2,0:T(8,128)S(1)}, u32[]{:S(2)}, u32[]{:S(2)}) collective-permute-start(f32[1,8,1,128]{3,1,2,0:T(8,128)S(1)} %get-tuple-element.55), channel_id=1, source_target_pairs={{1,0},{2,1},{3,2},{0,3},{5,4},{6,5},{7,6},{4,7},{9,8},{10,9},{11,1... | collective-permute-start | bytes 12296 | tf_op jit(solution)/shard_map/ppermute | solution.py:34
  38.6 3.1 %collective-permute-start.11 = (f32[1,8,1,128]{3,1,2,0:T(8,128)S(1)}, f32[1,8,1,128]{3,1,2,0:T(8,128)S(1)}, u32[]{:S(2)}, u32[]{:S(2)}) collective-permute-start(f32[1,8,1,128]{3,1,2,0:T(8,128)S(1)} %get-tuple-element.56), channel_id=1, source_target_pairs={{0,1},{1,2},{2,3},{3,0},{4,5},{5,6},{6,7},{7,4},{8,9},{9,10},{10,1... | collective-permute-start | bytes 12296 | tf_op jit(solution)/shard_map/ppermute | solution.py:33
  42.8 0.8 copy-start.11
  43.9 3.7 %collective-permute-start.12 = (f32[2,1,8,128]{3,1,2,0:T(1,128)S(1)}, f32[2,1,8,128]{3,1,2,0:T(1,128)S(1)}, u32[]{:S(2)}, u32[]{:S(2)}) collective-permute-start(f32[2,1,8,128]{3,1,2,0:T(1,128)S(1)} %get-tuple-element.33), channel_id=1, source_target_pairs={{4,0},{8,4},{12,8},{16,12},{20,16},{24,20},{28,24},{0,28},{5,1},{9... | collective-permute-start | bytes 24584 | tf_op jit(solution)/shard_map/ppermute | solution.py:34
  44.0 6.4 %collective-permute-start.13 = (f32[2,1,8,128]{3,1,2,0:T(1,128)S(1)}, f32[2,1,8,128]{3,1,2,0:T(1,128)S(1)}, u32[]{:S(2)}, u32[]{:S(2)}) collective-permute-start(f32[2,1,8,128]{3,1,2,0:T(1,128)S(1)} %get-tuple-element.34), channel_id=1, source_target_pairs={{0,4},{4,8},{8,12},{12,16},{16,20},{20,24},{24,28},{28,0},{1,5},{5... | collective-permute-start | bytes 24584 | tf_op jit(solution)/shard_map/ppermute | solution.py:33
  50.5 1.4 %collective-permute-start.14 = (f32[2,8,1,128]{3,1,2,0:T(8,128)S(1)}, f32[2,8,1,128]{3,1,2,0:T(8,128)S(1)}, u32[]{:S(2)}, u32[]{:S(2)}) collective-permute-start(f32[2,8,1,128]{3,1,2,0:T(8,128)S(1)} %get-tuple-element.31), channel_id=1, source_target_pairs={{1,0},{2,1},{3,2},{0,3},{5,4},{6,5},{7,6},{4,7},{9,8},{10,9},{11,1... | collective-permute-start | bytes 24584 | tf_op jit(solution)/shard_map/ppermute | solution.py:34
  50.5 3.2 %collective-permute-start.15 = (f32[2,8,1,128]{3,1,2,0:T(8,128)S(1)}, f32[2,8,1,128]{3,1,2,0:T(8,128)S(1)}, u32[]{:S(2)}, u32[]{:S(2)}) collective-permute-start(f32[2,8,1,128]{3,1,2,0:T(8,128)S(1)} %get-tuple-element.32), channel_id=1, source_target_pairs={{0,1},{1,2},{2,3},{3,0},{4,5},{5,6},{6,7},{7,4},{8,9},{9,10},{10,1... | collective-permute-start | bytes 24584 | tf_op jit(solution)/shard_map/ppermute | solution.py:33
  54.7 0.7 copy-start.4
  55.6 0.9 copy-start.3
  56.7 3.7 %collective-permute-start.16 = (f32[1,1,8,128]{3,1,2,0:T(1,128)S(1)}, f32[1,1,8,128]{3,1,2,0:T(1,128)S(1)}, u32[]{:S(2)}, u32[]{:S(2)}) collective-permute-start(f32[1,1,8,128]{3,1,2,0:T(1,128)S(1)} %get-tuple-element.49), channel_id=1, source_target_pairs={{4,0},{8,4},{12,8},{16,12},{20,16},{24,20},{28,24},{0,28},{5,1},{9... | collective-permute-start | bytes 12296 | tf_op jit(solution)/shard_map/ppermute | solution.py:34
  56.8 6.4 %collective-permute-start.17 = (f32[1,1,8,128]{3,1,2,0:T(1,128)S(1)}, f32[1,1,8,128]{3,1,2,0:T(1,128)S(1)}, u32[]{:S(2)}, u32[]{:S(2)}) collective-permute-start(f32[1,1,8,128]{3,1,2,0:T(1,128)S(1)} %get-tuple-element.50), channel_id=1, source_target_pairs={{0,4},{4,8},{8,12},{12,16},{16,20},{20,24},{24,28},{28,0},{1,5},{5... | collective-permute-start | bytes 12296 | tf_op jit(solution)/shard_map/ppermute | solution.py:33
  63.2 1.4 %collective-permute-start.18 = (f32[1,8,1,128]{3,1,2,0:T(8,128)S(1)}, f32[1,8,1,128]{3,1,2,0:T(8,128)S(1)}, u32[]{:S(2)}, u32[]{:S(2)}) collective-permute-start(f32[1,8,1,128]{3,1,2,0:T(8,128)S(1)} %get-tuple-element.47), channel_id=1, source_target_pairs={{1,0},{2,1},{3,2},{0,3},{5,4},{6,5},{7,6},{4,7},{9,8},{10,9},{11,1... | collective-permute-start | bytes 12296 | tf_op jit(solution)/shard_map/ppermute | solution.py:34
  63.3 3.1 %collective-permute-start.19 = (f32[1,8,1,128]{3,1,2,0:T(8,128)S(1)}, f32[1,8,1,128]{3,1,2,0:T(8,128)S(1)}, u32[]{:S(2)}, u32[]{:S(2)}) collective-permute-start(f32[1,8,1,128]{3,1,2,0:T(8,128)S(1)} %get-tuple-element.48), channel_id=1, source_target_pairs={{0,1},{1,2},{2,3},{3,0},{4,5},{5,6},{6,7},{7,4},{8,9},{9,10},{10,1... | collective-permute-start | bytes 12296 | tf_op jit(solution)/shard_map/ppermute | solution.py:33
  94.0 3.7 %collective-permute-start.20 = (f32[1,1,8,128]{3,1,2,0:T(1,128)S(1)}, f32[1,1,8,128]{3,1,2,0:T(1,128)S(1)}, u32[]{:S(2)}, u32[]{:S(2)}) collective-permute-start(f32[1,1,8,128]{3,1,2,0:T(1,128)S(1)} %get-tuple-element.41), channel_id=1, source_target_pairs={{4,0},{8,4},{12,8},{16,12},{20,16},{24,20},{28,24},{0,28},{5,1},{9... | collective-permute-start | bytes 12296 | tf_op jit(solution)/shard_map/ppermute | solution.py:34
  96.1 6.3 %collective-permute-start.21 = (f32[1,1,8,128]{3,1,2,0:T(1,128)S(1)}, f32[1,1,8,128]{3,1,2,0:T(1,128)S(1)}, u32[]{:S(2)}, u32[]{:S(2)}) collective-permute-start(f32[1,1,8,128]{3,1,2,0:T(1,128)S(1)} %get-tuple-element.42), channel_id=1, source_target_pairs={{0,4},{4,8},{8,12},{12,16},{16,20},{20,24},{24,28},{28,0},{1,5},{5... | collective-permute-start | bytes 12296 | tf_op jit(solution)/shard_map/ppermute | solution.py:33
  102.4 1.4 %collective-permute-start.22 = (f32[1,8,1,128]{3,1,2,0:T(8,128)S(1)}, f32[1,8,1,128]{3,1,2,0:T(8,128)S(1)}, u32[]{:S(2)}, u32[]{:S(2)}) collective-permute-start(f32[1,8,1,128]{3,1,2,0:T(8,128)S(1)} %get-tuple-element.39), channel_id=1, source_target_pairs={{1,0},{2,1},{3,2},{0,3},{5,4},{6,5},{7,6},{4,7},{9,8},{10,9},{11,1... | collective-permute-start | bytes 12296 | tf_op jit(solution)/shard_map/ppermute | solution.py:34
  102.5 3.1 %collective-permute-start.23 = (f32[1,8,1,128]{3,1,2,0:T(8,128)S(1)}, f32[1,8,1,128]{3,1,2,0:T(8,128)S(1)}, u32[]{:S(2)}, u32[]{:S(2)}) collective-permute-start(f32[1,8,1,128]{3,1,2,0:T(8,128)S(1)} %get-tuple-element.40), channel_id=1, source_target_pairs={{0,1},{1,2},{2,3},{3,0},{4,5},{5,6},{6,7},{7,4},{8,9},{9,10},{10,1... | collective-permute-start | bytes 12296 | tf_op jit(solution)/shard_map/ppermute | solution.py:33
  (4 other events, 2.7 us)
